TPU v7x, 64 devices: a 2x2x8 block of a 4x4x8 slice. The times are simulated.
64 devices in a mesh: rep: 4 (over x, y), dp: 16 (over z, core).
Axes of the slice: x: 2, y: 2, z: 8, core: 2. Of those that a mesh axis runs over, the one named last changes fastest.
The devices are a block of a 4x4x8 slice.
Arguments:
- g_w_gate: bfloat16 [64, 2, 512, 8192], P(('rep', 'dp')), parts along dimension 0
- g_w_up: bfloat16 [64, 2, 512, 8192], P(('rep', 'dp')), parts along dimension 0
- g_w_down: bfloat16 [64, 2, 8192, 512], P(('rep', 'dp')), parts along dimension 0
- w_gate: bfloat16 [2, 512, 8192], replicated
- w_up: bfloat16 [2, 512, 8192], replicated
- w_down: bfloat16 [2, 8192, 512], replicated
- m_w_gate: float32 [2, 512, 8192], P(None, 'dp')
- m_w_up: float32 [2, 512, 8192], P(None, 'dp')
- m_w_down: float32 [2, 8192, 512], P(None, 'dp')
- v_w_gate: float32 [2, 512, 8192], P(None, 'dp')
- v_w_up: float32 [2, 512, 8192], P(None, 'dp')
- v_w_down: float32 [2, 8192, 512], P(None, 'dp')
Outputs:
- output 1: bfloat16 [8, 512, 8192], P('rep'), parts along dimension 0
- output 2: bfloat16 [8, 512, 8192], P('rep'), parts along dimension 0
- output 3: bfloat16 [8, 8192, 512], P('rep'), parts along dimension 0
- output 4: float32 [8, 512, 8192], P('rep', 'dp'), parts along dimension 0
- output 5: float32 [8, 512, 8192], P('rep', 'dp'), parts along dimension 0
- output 6: float32 [8, 8192, 512], P('rep', 'dp'), parts along dimension 0
- output 7: float32 [8, 512, 8192], P('rep', 'dp'), parts along dimension 0
- output 8: float32 [8, 512, 8192], P('rep', 'dp'), parts along dimension 0
- output 9: float32 [8, 8192, 512], P('rep', 'dp'), parts along dimension 0
There are 4 independent parts. A program takes and returns all parts, laid end to end along the dimension named above; an argument that names none is the same for every part.
All inputs are finite; a program needn't handle non-finite values.
Results may differ from a plain program's by a relative error of at most 0.022.
Values are sent between devices in bfloat16 or wider.
A program may use at most 768 MiB of HBM per device.

v0:
```python
import jax
import jax.numpy as jnp
from jax import lax
from jax.sharding import PartitionSpec as P


def adamw(w, m, v, g):
    m = 0.9 * m + 0.1 * g
    v = 0.95 * v + 0.05 * g * g
    step = m * lax.rsqrt(v + 1e-8) + 0.1 * w
    return (w - 0.02 * step).astype(jnp.bfloat16), m, v


def solution(mesh):
    def step(*arrays):
        terms, weights, m, v = (arrays[i : i + 3] for i in (0, 3, 6, 9))
        gradients = [lax.psum_scatter(t[0], "dp", scatter_dimension=1, tiled=True).astype(jnp.float32) for t in terms]
        me = lax.axis_index("dp")
        own = [lax.dynamic_slice_in_dim(w, me * one.shape[1], one.shape[1], 1).astype(jnp.float32) for w, one in zip(weights, m, strict=True)]
        new = [adamw(w, m, v, g) for w, m, v, g in zip(own, m, v, gradients, strict=True)]
        whole = [lax.all_gather(one[0], "dp", axis=1, tiled=True) for one in new]
        return (*whole, *(one[1] for one in new), *(one[2] for one in new))

    all_of, cut = P(None, None, None), P(None, "dp", None)
    return jax.shard_map(
        step,
        mesh=mesh,
        in_specs=(P(("rep", "dp"), None, None, None),) * 3 + (all_of,) * 3 + (cut,) * 6,
        out_specs=(P("rep", None, None),) * 3 + (P("rep", "dp", None),) * 6,
        check_vma=False,
    )
```

profile of v0, /device:TPU:21, one launch (start us, length us, event | category | flops | bytes accessed | tf_op | source)
XLA Modules:
  0.0 628.4 jit_solution(10337094925266567556)
XLA Ops:
  7.2 0.1 reduce-scatter.8.cloned.1.call-start
  7.3 0.7 reduce-scatter.8.cloned.1.call-update
  8.0 0.1 reduce-scatter.6.cloned.1.call-start
  8.1 0.7 reduce-scatter.6.cloned.1.call-update
  8.8 0.1 reduce-scatter.4.cloned.1.call-start
  8.9 0.0 copy-start.1
  8.9 0.7 reduce-scatter.4.cloned.1.call-update
  9.6 0.1 all-gather.8.cloned.1.call-start
  9.7 102.0 %reduce-scatter.8.cloned.1.call-done = bf16[2,512,512]{2,1,0:T(8,128)(2,1)} async-done(((bf16[2,8192,512]{2,1,0:T(8,128)(2,1)}), bf16[2,512,512]{2,1,0:T(8,128)(2,1)}) %reduce-scatter.8.cloned.1.call-update) | async-done | bytes 1048592 | tf_op jit(solution)/shard_map/reduce_scatter | solution.py:17
  111.7 0.0 copy-done.1
  111.7 5.3 fusion.10
  117.0 0.1 all-gather.8.cloned.1.call-update
  117.1 0.1 all-gather.6.cloned.1.call-start
  117.1 92.9 %reduce-scatter.6.cloned.1.call-done = bf16[2,32,8192]{2,1,0:T(8,128)(2,1)} async-done(((bf16[2,512,8192]{2,1,0:T(8,128)(2,1)}), bf16[2,32,8192]{2,1,0:T(8,128)(2,1)}) %reduce-scatter.6.cloned.1.call-update) | async-done | bytes 1048592 | tf_op jit(solution)/shard_map/reduce_scatter | solution.py:17
  210.1 0.0 copy-start.2
  210.1 5.9 fusion.6
  215.9 0.1 all-gather.6.cloned.1.call-update
  216.0 0.1 all-gather.4.cloned.1.call-start
  216.0 92.4 %reduce-scatter.4.cloned.1.call-done = bf16[2,32,8192]{2,1,0:T(8,128)(2,1)} async-done(((bf16[2,512,8192]{2,1,0:T(8,128)(2,1)}), bf16[2,32,8192]{2,1,0:T(8,128)(2,1)}) %reduce-scatter.4.cloned.1.call-update) | async-done | bytes 1048592 | tf_op jit(solution)/shard_map/reduce_scatter | solution.py:17
  308.4 0.0 copy-done.2
  308.4 5.1 fusion.2
  313.5 0.1 all-gather.4.cloned.1.call-update
  313.6 88.6 %all-gather.8.cloned.1.call-done = bf16[2,8192,512]{2,1,0:T(8,128)(2,1)} async-done(((bf16[2,512,512]{2,1,0:T(8,128)(2,1)}), bf16[2,8192,512]{2,1,0:T(8,128)(2,1)}) %all-gather.8.cloned.1.call-update) | async-done | bytes 16777232 | tf_op jit(solution)/shard_map/all_gather | solution.py:21
  402.2 92.6 %all-gather.6.cloned.1.call-done = bf16[2,512,8192]{2,1,0:T(8,128)(2,1)} async-done(((bf16[2,32,8192]{2,1,0:T(8,128)(2,1)}), bf16[2,512,8192]{2,1,0:T(8,128)(2,1)}) %all-gather.6.cloned.1.call-update) | async-done | bytes 16777232 | tf_op jit(solution)/shard_map/all_gather | solution.py:21
  494.8 92.6 %all-gather.4.cloned.1.call-done = bf16[2,512,8192]{2,1,0:T(8,128)(2,1)} async-done(((bf16[2,32,8192]{2,1,0:T(8,128)(2,1)}), bf16[2,512,8192]{2,1,0:T(8,128)(2,1)}) %all-gather.4.cloned.1.call-update) | async-done | bytes 16777232 | tf_op jit(solution)/shard_map/all_gather | solution.py:21
  587.5 0.0 copy-start
  587.5 0.0 slice-start
  587.5 0.0 slice-start.1
  587.5 16.7 %copy.24 = bf16[2,512,8192]{2,1,0:T(8,128)(2,1)} copy(bf16[2,512,8192]{2,1,0:T(8,128)(2,1)} %all-gather.4.cloned.1.call-done) | data formatting | bytes 33554432
  604.2 0.0 copy-done
  604.2 0.0 slice-start.2
  604.2 0.0 slice-start.3
  604.2 8.5 %copy.25 = bf16[2,512,8192]{2,1,0:T(8,128)(2,1)} copy(bf16[2,512,8192]{2,1,0:T(8,128)(2,1)S(1)} %copy-done) | data formatting | bytes 33554432
  612.7 0.0 slice-done
  612.7 0.0 slice-done.1
  612.7 1.5 slice-done.2
  614.2 1.2 slice-done.3
  615.4 6.2 copy.26
  (1 shorter events, 0.0 us)
Async XLA Ops:
  7.2 104.5 %reduce-scatter.8.cloned.1.call-start = ((), (), s32[]{:S(2)}) async-start(), calls=%async_computation.7 | async-start | bytes 17825792 | tf_op jit(solution)/shard_map/reduce_scatter | solution.py:17
  8.0 202.1 %reduce-scatter.6.cloned.1.call-start = ((), (), s32[]{:S(2)}) async-start(), calls=%async_computation.5 | async-start | bytes 17825792 | tf_op jit(solution)/shard_map/reduce_scatter | solution.py:17
  8.8 299.6 %reduce-scatter.4.cloned.1.call-start = ((), (), s32[]{:S(2)}) async-start(), calls=%async_computation.3 | async-start | bytes 17825792 | tf_op jit(solution)/shard_map/reduce_scatter | solution.py:17
  8.9 102.9 %copy-start.1 = (f32[2,512,512]{2,1,0:T(8,128)S(1)}, f32[2,512,512]{2,1,0:T(8,128)}, u32[]{:S(2)}) copy-start(f32[2,512,512]{2,1,0:T(8,128)} %param.23) | copy-start | bytes 6291460
  9.6 392.6 %all-gather.8.cloned.1.call-start = ((), (), s32[]{:S(2)}) async-start(), calls=%async_computation.8 | async-start | bytes 17825792 | tf_op jit(solution)/shard_map/all_gather | solution.py:21
  117.1 377.8 %all-gather.6.cloned.1.call-start = ((), (), s32[]{:S(2)}) async-start(), calls=%async_computation.6 | async-start | bytes 17825792 | tf_op jit(solution)/shard_map/all_gather | solution.py:21
  210.1 98.4 %copy-start.2 = (f32[2,32,8192]{2,1,0:T(8,128)S(1)}, f32[2,32,8192]{2,1,0:T(8,128)}, u32[]{:S(2)}) copy-start(f32[2,32,8192]{2,1,0:T(8,128)} %param.21) | copy-start | bytes 6291460
  216.0 371.5 %all-gather.4.cloned.1.call-start = ((), (), s32[]{:S(2)}) async-start(), calls=%async_computation.4 | async-start | bytes 17825792 | tf_op jit(solution)/shard_map/all_gather | solution.py:21
  587.5 16.7 %copy-start = (bf16[2,512,8192]{2,1,0:T(8,128)(2,1)S(1)}, bf16[2,512,8192]{2,1,0:T(8,128)(2,1)}, u32[]{:S(2)}) copy-start(bf16[2,512,8192]{2,1,0:T(8,128)(2,1)} %all-gather.6.cloned.1.call-done) | copy-start | bytes 50331652
  587.5 25.2 %slice-start = ((s8[16777216]{0:T(1024)(128)(4,1)}), s8[4194304]{0:T(1024)(128)(4,1)S(1)}, s32[]{:S(2)}) async-start(s8[16777216]{0:T(1024)(128)(4,1)} %bitcast.6), calls=%async_computation.9 | async-start | bytes 8388608
  587.5 25.2 %slice-start.1 = ((s8[16777216]{0:T(1024)(128)(4,1)}), s8[4194304]{0:T(1024)(128)(4,1)S(1)}, s32[]{:S(2)}) async-start(s8[16777216]{0:T(1024)(128)(4,1)} %bitcast.6), calls=%async_computation.10 | async-start | bytes 8388608
  604.2 10.0 %slice-start.2 = ((s8[16777216]{0:T(1024)(128)(4,1)}), s8[4194304]{0:T(1024)(128)(4,1)S(1)}, s32[]{:S(2)}) async-start(s8[16777216]{0:T(1024)(128)(4,1)} %bitcast.6), calls=%async_computation.11 | async-start | bytes 8388608
  604.2 11.2 %slice-start.3 = ((s8[16777216]{0:T(1024)(128)(4,1)}), s8[4194304]{0:T(1024)(128)(4,1)S(1)}, s32[]{:S(2)}) async-start(s8[16777216]{0:T(1024)(128)(4,1)} %bitcast.6), calls=%async_computation.12 | async-start | bytes 8388608
Sparse Core Ops, SparseCore 0:
  10.4 101.3 reduce-scatter.7
  114.1 95.9 reduce-scatter.5
  212.4 95.9 reduce-scatter.3
  310.5 91.6 all-gather.7
  404.3 90.5 all-gather.5
  496.9 90.5 all-gather.3
where the time goes:
time: 629 us; the launch traced here: 628 us
  waiting for transfers between devices  564 us (90%)
  local copies, waits for them, and re-layouts  34.1 us (5%)
  other arithmetic  16.2 us (3%)
  between operations  14.2 us (2%)
    reduce_scatter x3, waiting for transfers between devices, step(): lax.psum_scatter(t[0], 'dp', scatter_dimension=1, tiled=True)  287 us
    all_gather x3, waiting for transfers between devices, step(): whole = [lax.all_gather(one[0], 'dp', axis=1, tiled=True) for one in new]  274 us
    unnamed x17, local copies, waits for them, and re-layouts  34.1 us
    convert_element_type x3, other arithmetic, adamw(): return ((w - 0.02 * step).astype(jnp.bfloat16), m, v)  16.2 us
  transfers between devices with their start and end apart: 6, of which 6 were waited for; matrix products, arithmetic and copies ran while one was open for 3% of the time, Pallas kernels for 0%

commit v1 on v0

v1 whole, which is shorter than its diff:
```python
import functools

import jax
import jax.numpy as jnp
from jax import lax
from jax.experimental import pallas as pl
from jax.experimental.pallas import tpu as pltpu
from jax.sharding import PartitionSpec as P

CORES = 2
LAYERS = 2
NAMES = 3
CHUNK = 32768
MESH = pl.DeviceIdType.MESH


def adamw(w, m, v, g):
    m = 0.9 * m + 0.1 * g
    v = 0.95 * v + 0.05 * g * g
    step = m * lax.rsqrt(v + 1e-8) + 0.1 * w
    return (w - 0.02 * step).astype(jnp.bfloat16), m, v


def chunks(shape, body):
    rows, columns = shape
    if columns * rows <= CHUNK:
        body((slice(None), slice(None)))
    elif rows * 128 <= CHUNK and columns % (CHUNK // rows) == 0:
        size = CHUNK // rows

        @pl.loop(0, columns // size)
        def _(i):
            body((slice(None), pl.ds(pl.multiple_of(i * size, size), size)))
    else:
        size = CHUNK // columns

        @pl.loop(0, rows // size)
        def _(i):
            body((pl.ds(pl.multiple_of(i * size, size), size), slice(None)))


def kernel(n, *refs):
    groups = [refs[i : i + NAMES] for i in range(0, 12 * NAMES, NAMES)]
    g, w, m, v, whole, new_m, new_v, slots, theirs, own, m_buf, v_buf = groups
    rs_send, rs_recv, pt_send, pt_recv, own_sem, mv_sem, out_sem, ag_send, ag_recv, pa_send, pa_recv = refs[12 * NAMES :]
    chips = n // CORES
    last = chips - 1
    me = lax.axis_index("dp")
    core, chip = lax.rem(me, CORES), me // CORES
    partner = me + 1 - 2 * core
    up, down = lax.rem(me + CORES, n), lax.rem(me + n - CORES, n)
    to = (up, down)
    pieces = [(d, j) for j in range(NAMES) for d in range(LAYERS)]

    def rows(j, device):
        size = m[j].shape[1]
        return pl.ds(pl.multiple_of(device * size, size), size)

    def rs_chip(d, k):
        return lax.rem(chip + 2 * chips - 1 - k, chips) if d == 0 else lax.rem(chip + 1 + k, chips)

    def ag_chip(d, k):
        return lax.rem(chip + chips - k, chips) if d == 0 else lax.rem(chip + k, chips)

    def remote(src, dst, send, recv, device):
        return pltpu.make_async_remote_copy(src_ref=src, dst_ref=dst, send_sem=send, recv_sem=recv, device_id={"dp": device}, device_id_type=MESH)

    def to_partner(d, j, k):
        block = rows(j, rs_chip(d, k) * CORES + 1 - core)
        return remote(g[j].at[0, d, block], theirs[j].at[d, k], pt_send.at[d, j, k], pt_recv.at[d, j, k], partner)

    def load_own(d, j, k):
        block = rows(j, rs_chip(d, k) * CORES + core)
        half = lax.rem(k, 2)
        return pltpu.make_async_copy(g[j].at[0, d, block], own[j].at[d, half], own_sem.at[d, j, half])

    def load_w(d, j):
        half = (last + 1) % 2
        return pltpu.make_async_copy(w[j].at[d, rows(j, me)], own[j].at[d, half], own_sem.at[d, j, half])

    def ring(d, j, k):
        return remote(slots[j].at[d, k], slots[j].at[d, k + 1], rs_send.at[d, j, k], rs_recv.at[d, j, k + 1], to[d])

    def moments_in(d, j):
        return (
            pltpu.make_async_copy(m[j].at[d], m_buf[j], mv_sem.at[j, 0]),
            pltpu.make_async_copy(v[j].at[d], v_buf[j], mv_sem.at[j, 1]),
        )

    def moments_out(d, j):
        return (
            pltpu.make_async_copy(m_buf[j], new_m[j].at[d], mv_sem.at[j, 2]),
            pltpu.make_async_copy(v_buf[j], new_v[j].at[d], mv_sem.at[j, 3]),
        )

    def pass_on(d, j, k, src, block):
        return remote(src, whole[j].at[d, block], ag_send.at[d, j, k], ag_recv.at[d, j, k + 1], to[d])

    def share(d, j, k, src, block):
        return remote(src, whole[j].at[d, block], pa_send.at[d, j, k], pa_recv.at[d, j, k], partner)

    def keep(d, j):
        return pltpu.make_async_copy(slots[j].at[d, last], whole[j].at[d, rows(j, me)], out_sem.at[d, j])

    barrier = pltpu.get_barrier_semaphore()
    for device in (up, down, partner):
        pl.semaphore_signal(barrier, inc=1, device_id={"dp": device}, device_id_type=MESH)
    for d, j in pieces:
        load_own(d, j, 0).start()
    pl.semaphore_wait(barrier, 3)

    for k in range(2):
        for d, j in pieces:
            to_partner(d, j, k).start()

    def add(d, j, k, first):
        half = lax.rem(k, 2)

        def body(at):
            total = own[j][(d, half, *at)].astype(jnp.float32) + theirs[j][(d, k, *at)].astype(jnp.float32)
            if not first:
                total = total + slots[j][(d, k, *at)].astype(jnp.float32)
            slots[j][(d, k, *at)] = total.astype(jnp.bfloat16)

        chunks(own[j].shape[2:], body)

    def stage(k, first):
        for d, j in pieces:
            load_own(d, j, k + 1).start()
        for d, j in pieces:
            load_own(d, j, k).wait()
            to_partner(d, j, k).wait_recv()
            if not first:
                ring(d, j, k - 1).wait_recv()
            add(d, j, k, first)
            ring(d, j, k).start()

    stage(0, True)

    @pl.loop(1, last)
    def _(k):
        for d, j in pieces:
            to_partner(d, j, k + 1).start()
        stage(k, False)

    for d, j in pieces:
        load_w(d, j).start()
    for d, j in pieces:
        if d == 0:
            for copy in moments_in(d, j):
                copy.start()
    for d, j in pieces:
        load_own(d, j, last).wait()
        to_partner(d, j, last).wait_recv()
        load_w(d, j).wait()
        for copy in moments_in(d, j):
            copy.wait()
        ring(d, j, last - 1).wait_recv()

        def step(at, d=d, j=j):
            total = own[j][(d, last % 2, *at)].astype(jnp.float32) + theirs[j][(d, last, *at)].astype(jnp.float32)
            total = (total + slots[j][(d, last, *at)].astype(jnp.float32)).astype(jnp.bfloat16).astype(jnp.float32)
            new, m_buf[j][at], v_buf[j][at] = adamw(own[j][(d, (last + 1) % 2, *at)].astype(jnp.float32), m_buf[j][at], v_buf[j][at], total)
            slots[j][(d, last, *at)] = new

        chunks(own[j].shape[2:], step)
        for copy in moments_out(d, j):
            copy.start()
        mine = slots[j].at[d, last]
        pass_on(d, j, 0, mine, rows(j, me)).start()
        share(d, j, 0, mine, rows(j, me)).start()
        keep(d, j).start()
        for copy in moments_out(d, j):
            copy.wait()
        if d + 1 < LAYERS:
            for copy in moments_in(d + 1, j):
                copy.start()

    def gather(k, more):
        for d, j in pieces:
            block = rows(j, ag_chip(d, k) * CORES + core)
            here = whole[j].at[d, block]
            pass_on(d, j, k - 1, here, block).wait_recv()
            if more:
                pass_on(d, j, k, here, block).start()
            share(d, j, k, here, block).start()

    @pl.loop(1, last)
    def _(k):
        gather(k, True)

    gather(last, False)

    for d, j in pieces:
        keep(d, j).wait()

    @pl.loop(0, chips)
    def _(k):
        for d, j in pieces:
            block = rows(j, ag_chip(d, k) * CORES + core)
            here = whole[j].at[d, block]
            to_partner(d, j, k).wait_send()
            share(d, j, k, here, block).wait_send()
            share(d, j, k, here, block).wait_recv()

    @pl.loop(0, last)
    def _(k):
        for d, j in pieces:
            block = rows(j, ag_chip(d, k) * CORES + core)
            ring(d, j, k).wait_send()
            pass_on(d, j, k, whole[j].at[d, block], block).wait_send()


def solution(mesh):
    n = mesh.shape["dp"]
    chips = n // CORES

    def step(*arrays):
        terms, weights, m, v = (arrays[i : i + NAMES] for i in range(0, 4 * NAMES, NAMES))
        blocks = [one.shape[1:] for one in m]
        sems = lambda *shape: pltpu.SemaphoreType.DMA(shape)
        full = sems(LAYERS, NAMES, chips)
        any_space = pl.BlockSpec(memory_space=pl.ANY)
        out = pl.pallas_call(
            functools.partial(kernel, n),
            out_shape=[jax.ShapeDtypeStruct(one.shape, one.dtype) for one in (*weights, *m, *v)],
            in_specs=[any_space] * (4 * NAMES),
            out_specs=[any_space] * (3 * NAMES),
            scratch_shapes=[
                *(pltpu.VMEM((LAYERS, chips, *b), jnp.bfloat16) for b in blocks),
                *(pltpu.VMEM((LAYERS, chips, *b), jnp.bfloat16) for b in blocks),
                *(pltpu.VMEM((LAYERS, 2, *b), jnp.bfloat16) for b in blocks),
                *(pltpu.VMEM(b, jnp.float32) for b in blocks),
                *(pltpu.VMEM(b, jnp.float32) for b in blocks),
                full, full, full, full,
                sems(LAYERS, NAMES, 2), sems(NAMES, 4), sems(LAYERS, NAMES),
                full, full, full, full,
            ],
            compiler_params=pltpu.CompilerParams(collective_id=0, has_side_effects=True, vmem_limit_bytes=67_043_328),
            name="step",
        )(*terms, *weights, *m, *v)
        return tuple(out)

    all_of, cut = P(None, None, None), P(None, "dp", None)
    return jax.shard_map(
        step,
        mesh=mesh,
        in_specs=(P(("rep", "dp"), None, None, None),) * 3 + (all_of,) * 3 + (cut,) * 6,
        out_specs=(P("rep", None, None),) * 3 + (P("rep", "dp", None),) * 6,
        check_vma=False,
    )
```

time: 629 us -> 538 us (0.86)
  waiting for transfers between devices: 564 us -> 0 us
  Pallas kernels: 0 us -> 490 us
  other arithmetic: 16.2 us -> 0.01 us
  between operations: 14.2 us -> 0.7 us
  local copies, waits for them, and re-layouts: 34.1 us -> 47.2 us
    pallas_call x0 -> x1, Pallas kernels: none -> 490 us  [step(): pl.pallas_call(functools.partial(kernel, n), out_shape=[jax.ShapeDtypeStr...]
    reduce_scatter x3 -> x0, waiting for transfers between devices: 287 us -> none  [step(): lax.psum_scatter(t[0], 'dp', scatter_dimension=1, tiled=True)]
    all_gather x3 -> x0, waiting for transfers between devices: 274 us -> none  [step(): whole = [lax.all_gather(one[0], 'dp', axis=1, tiled=True) for one in new]]
    convert_element_type x3 -> x0, other arithmetic: 16.2 us -> none  [adamw(): return ((w - 0.02 * step).astype(jnp.bfloat16), m, v)]
    unnamed x17 -> x31, local copies, waits for them, and re-layouts: 34.1 us -> 47.2 us
  transfers between devices with their start and end apart: 6 -> 0, of which waited for: 6 -> 0; matrix products, arithmetic and copies ran while one was open for 3% -> 0% of each run, Pallas kernels for 0% -> 0%
where the time goes in v1:
time: 538 us
  Pallas kernels  490 us (91%)
  local copies, waits for them, and re-layouts  47.2 us (9%)
    pallas_call x1, Pallas kernels, step(): pl.pallas_call(functools.partial(kernel, n), out_shape=[jax.ShapeDtypeStr...  490 us
    unnamed x31, local copies, waits for them, and re-layouts  47.2 us

profile of v1, /device:TPU:21, one launch (start us, length us, event | category | flops | bytes accessed | tf_op | source)
XLA Modules:
  0.0 538.1 jit_solution(17401160867322004956)
XLA Ops:
  0.6 490.2 %step.1 = (bf16[2,512,8192]{2,1,0:T(8,128)(2,1)}, bf16[2,512,8192]{2,1,0:T(8,128)(2,1)}, bf16[2,8192,512]{2,1,0:T(8,128)(2,1)}, f32[2,32,8192]{2,1,0:T(8,128)}, ...) custom-call(bf16[1,2,512,8192]{3,2,1,0:T(8,128)(2,1)} %refs_0_.1, ...), custom_call_target="tpu_custom_call" | custom-call | tf_op jit(solution)/shard_map/step/pallas_call | solution.py:224
  490.8 0.0 copy-start
  490.8 0.0 slice-start
  490.9 0.0 slice-start.1
  490.9 16.7 %copy.30 = bf16[2,512,8192]{2,1,0:T(8,128)(2,1)} copy(bf16[2,512,8192]{2,1,0:T(8,128)(2,1)} %get-tuple-element.18) | data formatting | bytes 33554432
  507.6 0.0 copy-done
  507.6 0.0 slice-start.2
  507.6 0.0 slice-start.3
  507.6 8.5 %copy.31 = bf16[2,512,8192]{2,1,0:T(8,128)(2,1)} copy(bf16[2,512,8192]{2,1,0:T(8,128)(2,1)S(1)} %copy-done) | data formatting | bytes 33554432
  516.1 0.0 slice-done
  516.1 0.0 slice-done.1
  516.1 1.5 slice-done.2
  517.6 1.2 slice-done.3
  518.7 0.0 copy-start.6
  518.7 6.3 %copy.32 = bf16[2,8192,512]{2,1,0:T(8,128)(2,1)} copy(bf16[2,8192,512]{2,1,0:T(8,128)(2,1)S(1)} %bitcast.1) | data formatting | bytes 33554432
  525.0 0.0 copy-done.6
  525.0 0.0 copy-start.5
  525.0 1.3 copy.33
  526.4 1.0 copy-done.5
  527.4 0.0 copy-start.4
  527.4 1.3 copy.34
  528.7 1.0 copy-done.4
  529.7 0.0 copy-start.3
  529.7 1.3 copy.35
  531.1 1.0 copy-done.3
  532.1 0.0 copy-start.2
  532.1 1.3 copy.36
  533.4 1.0 copy-done.2
  534.4 0.0 copy-start.1
  534.4 1.3 copy.37
  535.8 1.0 copy-done.1
  536.8 1.3 copy.38
  (1 shorter events, 0.0 us)
Async XLA Ops:
  490.8 16.7 %copy-start = (bf16[2,512,8192]{2,1,0:T(8,128)(2,1)S(1)}, bf16[2,512,8192]{2,1,0:T(8,128)(2,1)}, u32[]{:S(2)}) copy-start(bf16[2,512,8192]{2,1,0:T(8,128)(2,1)} %get-tuple-element.19) | copy-start | bytes 50331652
  490.8 25.2 %slice-start = ((s8[16777216]{0:T(1024)(128)(4,1)}), s8[4194304]{0:T(1024)(128)(4,1)S(1)}, s32[]{:S(2)}) async-start(s8[16777216]{0:T(1024)(128)(4,1)} %bitcast), calls=%async_computation | async-start | bytes 8388608
  490.9 25.2 %slice-start.1 = ((s8[16777216]{0:T(1024)(128)(4,1)}), s8[4194304]{0:T(1024)(128)(4,1)S(1)}, s32[]{:S(2)}) async-start(s8[16777216]{0:T(1024)(128)(4,1)} %bitcast), calls=%async_computation.1 | async-start | bytes 8388608
  507.6 10.0 %slice-start.2 = ((s8[16777216]{0:T(1024)(128)(4,1)}), s8[4194304]{0:T(1024)(128)(4,1)S(1)}, s32[]{:S(2)}) async-start(s8[16777216]{0:T(1024)(128)(4,1)} %bitcast), calls=%async_computation.2 | async-start | bytes 8388608
  507.6 11.2 %slice-start.3 = ((s8[16777216]{0:T(1024)(128)(4,1)}), s8[4194304]{0:T(1024)(128)(4,1)S(1)}, s32[]{:S(2)}) async-start(s8[16777216]{0:T(1024)(128)(4,1)} %bitcast), calls=%async_computation.3 | async-start | bytes 8388608
  518.7 6.3 %copy-start.6 = (f32[2,32,8192]{2,1,0:T(8,128)S(1)}, f32[2,32,8192]{2,1,0:T(8,128)}, u32[]{:S(2)}) copy-start(f32[2,32,8192]{2,1,0:T(8,128)} %get-tuple-element.21) | copy-start | bytes 6291460
  525.0 2.3 copy-start.5
  527.4 2.3 copy-start.4
  529.7 2.3 copy-start.3
  532.1 2.3 copy-start.2
  534.4 2.3 copy-start.1

commit v2 on v0

v2 whole, which is shorter than its diff:
```python
import functools

import jax
import jax.numpy as jnp
from jax import lax
from jax.experimental import pallas as pl
from jax.experimental.pallas import tpu as pltpu
from jax.sharding import PartitionSpec as P

CORES = 2
LAYERS = 2
NAMES = 3
CHUNK = 32768
VMEM_LIMIT = 4_000_000
MESH = pl.DeviceIdType.MESH


def adamw(w, m, v, g):
    m = 0.9 * m + 0.1 * g
    v = 0.95 * v + 0.05 * g * g
    step = m * lax.rsqrt(v + 1e-8) + 0.1 * w
    return (w - 0.02 * step).astype(jnp.bfloat16), m, v


def chunks(shape, body):
    rows, columns = shape
    if columns * rows <= CHUNK:
        body((slice(None), slice(None)))
    elif rows * 128 <= CHUNK and columns % (CHUNK // rows) == 0:
        size = CHUNK // rows

        @pl.loop(0, columns // size)
        def _(i):
            body((slice(None), pl.ds(pl.multiple_of(i * size, size), size)))
    else:
        size = CHUNK // columns

        @pl.loop(0, rows // size)
        def _(i):
            body((pl.ds(pl.multiple_of(i * size, size), size), slice(None)))


def spot(place, at):
    layer, block = place
    row, column = at
    if isinstance(row, slice):
        return layer, block, column
    return layer, pl.ds(pl.multiple_of(block.start + row.start, row.size), row.size), column


def kernel(n, *refs):
    g, w, m, v, whole, new_m, new_v, own = (refs[i : i + NAMES] for i in range(0, 8 * NAMES, NAMES))
    rs_send, rs_recv, pt_send, pt_recv, own_sem, mv_sem, w_sem, ag_send, ag_recv, pa_send, pa_recv, free, pt_free = refs[8 * NAMES :]
    chips = n // CORES
    last = chips - 1
    me = lax.axis_index("dp")
    core, chip = lax.rem(me, CORES), me // CORES
    partner = me + 1 - 2 * core
    up, down = lax.rem(me + CORES, n), lax.rem(me + n - CORES, n)
    to, source = (up, down), (down, up)
    pieces = [(d, j) for j in range(NAMES) for d in range(LAYERS)]

    def rows(j, of_chip, of_core):
        size = m[j].shape[1]
        return pl.ds(pl.multiple_of((of_chip * CORES + of_core) * size, size), size)

    def sum_chip(d, k):
        return lax.rem(chip + 2 * chips - 1 - k, chips) if d == 0 else lax.rem(chip + 1 + k, chips)

    def place(d, j, k):
        return d, rows(j, lax.rem(chip + chips - k, chips) if d == 0 else lax.rem(chip + k, chips), core)

    def their_place(d, j, k):
        return d, rows(j, lax.rem(chip + chips - k, chips) if d == 0 else lax.rem(chip + k, chips), 1 - core)

    def remote(src, dst, send, recv, device):
        return pltpu.make_async_remote_copy(src_ref=src, dst_ref=dst, send_sem=send, recv_sem=recv, device_id={"dp": device}, device_id_type=MESH)

    def to_partner(d, j, k):
        block = rows(j, sum_chip(d, k), 1 - core)
        return remote(g[j].at[0, d, block], whole[j].at[place(d, j, k)], pt_send.at[d, j, k], pt_recv.at[d, j, k], partner)

    def load_own(d, j, k):
        return pltpu.make_async_copy(g[j].at[0, d, rows(j, sum_chip(d, k), core)], own[j].at[d], own_sem.at[d, j])

    def load_w(d, j):
        return pltpu.make_async_copy(w[j].at[d, rows(j, chip, core)], whole[j].at[place(d, j, 0)], w_sem.at[d, j])

    def load_moments(d, j):
        return (
            pltpu.make_async_copy(m[j].at[d], new_m[j].at[d], mv_sem.at[d, j, 0]),
            pltpu.make_async_copy(v[j].at[d], new_v[j].at[d], mv_sem.at[d, j, 1]),
        )

    def ring(d, j, k):
        here = whole[j].at[place(d, j, k)]
        return remote(here, here, rs_send.at[d, j, k], rs_recv.at[d, j, k + 1], to[d])

    def pass_on(d, j, k):
        here = whole[j].at[place(d, j, k)]
        return remote(here, here, ag_send.at[d, j, k], ag_recv.at[d, j, k + 1], to[d])

    def share(d, j, k):
        here = whole[j].at[place(d, j, k)]
        return remote(here, here, pa_send.at[d, j, k], pa_recv.at[d, j, k], partner)

    def allow(d, j, places):
        pl.semaphore_signal(free.at[d, j], inc=places, device_id={"dp": source[d]}, device_id_type=MESH)

    def allow_partner(d, j):
        pl.semaphore_signal(pt_free.at[d, j], inc=1, device_id={"dp": partner}, device_id_type=MESH)

    barrier = pltpu.get_barrier_semaphore()
    for device in (up, down, partner):
        pl.semaphore_signal(barrier, inc=1, device_id={"dp": device}, device_id_type=MESH)
    for d, j in pieces:
        load_own(d, j, 0).start()
    pl.semaphore_wait(barrier, 3)

    def add(d, j, k, first):
        here, there = place(d, j, k), their_place(d, j, k)

        def body(at):
            total = own[j][(d, *at)].astype(jnp.float32) + whole[j][spot(there, at)].astype(jnp.float32)
            if not first:
                total = total + whole[j][spot(here, at)].astype(jnp.float32)
            whole[j][spot(here, at)] = total.astype(jnp.bfloat16)

        chunks(own[j].shape[1:], body)

    def stage(k, first=False, lag=True):
        for d, j in pieces:
            to_partner(d, j, k + 1).start()
        for d, j in pieces:
            load_own(d, j, k).wait()
            to_partner(d, j, k).wait_recv()
            if not first:
                ring(d, j, k - 1).wait_recv()
            add(d, j, k, first)
            load_own(d, j, k + 1).start()
            ring(d, j, k).start()
            allow_partner(d, j)
            if lag:
                ring(d, j, k - 2).wait_send()
                allow(d, j, 1)

    for d, j in pieces:
        to_partner(d, j, 0).start()
    stage(0, first=True, lag=False)
    stage(1, lag=False)
    for d, j in pieces:
        for copy in load_moments(d, j):
            copy.start()

    @pl.loop(2, last)
    def _(k):
        stage(k)

    for d, j in pieces:
        load_w(d, j).start()
    for d, j in pieces:
        load_own(d, j, last).wait()
        to_partner(d, j, last).wait_recv()
        load_w(d, j).wait()
        for copy in load_moments(d, j):
            copy.wait()
        ring(d, j, last - 1).wait_recv()
        mine, here, there = place(d, j, 0), place(d, j, last), their_place(d, j, last)

        def step(at, d=d, j=j, mine=mine, here=here, there=there):
            total = own[j][(d, *at)].astype(jnp.float32) + whole[j][spot(there, at)].astype(jnp.float32)
            total = (total + whole[j][spot(here, at)].astype(jnp.float32)).astype(jnp.bfloat16).astype(jnp.float32)
            new, new_m[j][(d, *at)], new_v[j][(d, *at)] = adamw(
                whole[j][spot(mine, at)].astype(jnp.float32), new_m[j][(d, *at)], new_v[j][(d, *at)], total
            )
            whole[j][spot(mine, at)] = new

        chunks(own[j].shape[1:], step)
        allow_partner(d, j)
        ring(d, j, last - 2).wait_send()
        allow(d, j, 1)
        pl.semaphore_wait(free.at[d, j], 2)
        pass_on(d, j, 0).start()
        pl.semaphore_wait(pt_free.at[d, j], 1)
        share(d, j, 0).start()

    def gather(k, more=True, lag=False):
        for d, j in pieces:
            pass_on(d, j, k - 1).wait_recv()
            if more:
                pl.semaphore_wait(free.at[d, j], 1)
                pass_on(d, j, k).start()
            pl.semaphore_wait(pt_free.at[d, j], 1)
            share(d, j, k).start()
            if lag:
                ring(d, j, last - 1).wait_send()
                allow(d, j, 2)

    gather(1, lag=True)

    @pl.loop(2, last)
    def _(k):
        gather(k)

    gather(last, more=False)

    @pl.loop(0, chips)
    def _(k):
        for d, j in pieces:
            to_partner(d, j, k).wait_send()
            share(d, j, k).wait_send()
            share(d, j, k).wait_recv()

    @pl.loop(0, last)
    def _(k):
        for d, j in pieces:
            pass_on(d, j, k).wait_send()


def finish(*refs):
    count = len(refs[:-1]) // 2
    copies = [pltpu.make_async_copy(refs[i], refs[count + i], refs[-1].at[i]) for i in range(count)]
    for copy in copies:
        copy.start()
    for copy in copies:
        copy.wait()


def solution(mesh):
    n = mesh.shape["dp"]
    chips = n // CORES

    def step(*arrays):
        terms, weights, m, v = (arrays[i : i + NAMES] for i in range(0, 4 * NAMES, NAMES))
        blocks = [one.shape[1:] for one in m]
        sems = lambda *shape: pltpu.SemaphoreType.DMA(shape)
        full = sems(LAYERS, NAMES, chips)
        credits = pltpu.SemaphoreType.REGULAR((LAYERS, NAMES))
        any_space, vmem = (pl.BlockSpec(memory_space=space) for space in (pl.ANY, pltpu.VMEM))
        results = (*weights, *m, *v)
        out = pl.pallas_call(
            functools.partial(kernel, n),
            out_shape=[pltpu.VMEM(one.shape, one.dtype) for one in results],
            in_specs=[any_space] * (4 * NAMES),
            out_specs=[vmem] * (3 * NAMES),
            scratch_shapes=[
                *(pltpu.VMEM((LAYERS, *b), jnp.bfloat16) for b in blocks),
                full, full, full, full,
                sems(LAYERS, NAMES), sems(LAYERS, NAMES, 2), sems(LAYERS, NAMES),
                full, full, full, full,
                credits, credits,
            ],
            compiler_params=pltpu.CompilerParams(collective_id=0, has_side_effects=True, vmem_limit_bytes=VMEM_LIMIT),
            name="step",
        )(*terms, *weights, *m, *v)
        return tuple(
            pl.pallas_call(
                finish,
                out_shape=[jax.ShapeDtypeStruct(one.shape, one.dtype) for one in results],
                in_specs=[vmem] * (3 * NAMES),
                out_specs=[any_space] * (3 * NAMES),
                scratch_shapes=[sems(3 * NAMES)],
                compiler_params=pltpu.CompilerParams(vmem_limit_bytes=VMEM_LIMIT),
                name="finish",
            )(*(pltpu.with_memory_space_constraint(one, pltpu.VMEM) for one in out))
        )

    all_of, cut = P(None, None, None), P(None, "dp", None)
    return jax.shard_map(
        step,
        mesh=mesh,
        in_specs=(P(("rep", "dp"), None, None, None),) * 3 + (all_of,) * 3 + (cut,) * 6,
        out_specs=(P("rep", None, None),) * 3 + (P("rep", "dp", None),) * 6,
        check_vma=False,
    )
```

time: 629 us -> 511 us (0.81)
  waiting for transfers between devices: 564 us -> 0 us
  Pallas kernels: 0 us -> 510 us
  local copies, waits for them, and re-layouts: 34.1 us -> 0 us
  other arithmetic: 16.2 us -> 0 us
  between operations: 14.2 us -> 0.65 us
    pallas_call x0 -> x2, Pallas kernels: none -> 510 us  [the longest x1 490 us: step(): pl.pallas_call(functools.partial(kernel, n), out_shape=[pltpu.VMEM(one.sh...]
    reduce_scatter x3 -> x0, waiting for transfers between devices: 287 us -> none  [step(): lax.psum_scatter(t[0], 'dp', scatter_dimension=1, tiled=True)]
    all_gather x3 -> x0, waiting for transfers between devices: 274 us -> none  [step(): whole = [lax.all_gather(one[0], 'dp', axis=1, tiled=True) for one in new]]
    unnamed x17 -> x0, local copies, waits for them, and re-layouts: 34.1 us -> none
    convert_element_type x3 -> x0, other arithmetic: 16.2 us -> none  [adamw(): return ((w - 0.02 * step).astype(jnp.bfloat16), m, v)]
  transfers between devices with their start and end apart: 6 -> 0, of which waited for: 6 -> 0; matrix products, arithmetic and copies ran while one was open for 3% -> 0% of each run, Pallas kernels for 0% -> 0%
where the time goes in v2:
time: 511 us
  Pallas kernels  510 us (100%)
    pallas_call x1, Pallas kernels, step(): pl.pallas_call(functools.partial(kernel, n), out_shape=[pltpu.VMEM(one.sh...  490 us
    pallas_call x1, Pallas kernels, step(): pl.pallas_call(finish, out_shape=[jax.ShapeDtypeStruct(one.shape, one.dty...  20.2 us

profile of v2, /device:TPU:21, one launch (start us, length us, event | category | flops | bytes accessed | tf_op | source)
XLA Modules:
  0.0 511.1 jit_solution(13916171426468974963)
XLA Ops:
  0.6 490.2 %step.1 = (bf16[2,512,8192]{2,1,0:T(8,128)(2,1)S(1)}, bf16[2,512,8192]{2,1,0:T(8,128)(2,1)S(1)}, bf16[2,8192,512]{2,1,0:T(8,128)(2,1)S(1)}, f32[2,32,8192]{2,1,0...) custom-call(bf16[1,2,512,8192]{3,2,1,0:T(8,128)(2,1)} %refs_0_.1, ...), custom_call_target="tpu_custom_call" | custom-call | tf_op jit(solution)/shard_map/step/pallas_call | solution.py:241
  490.9 20.2 %finish.1 = (bf16[2,512,8192]{2,1,0:T(8,128)(2,1)}, bf16[2,512,8192]{2,1,0:T(8,128)(2,1)}, bf16[2,8192,512]{2,1,0:T(8,128)(2,1)}, f32[2,32,8192]{2,1,0:T(8,128)}...) custom-call(bf16[2,512,8192]{2,1,0:T(8,128)(2,1)S(1)} %get-tuple-ele, ...), custom_call_target="tpu_custom_call" | custom-call | tf_op jit(solution)/shard_map/finish/pallas_call | solution.py:257

commit v3 on v2

--- a/solution.py
+++ b/solution.py
@@ -7,9 +7,11 @@
 from jax.experimental.pallas import tpu as pltpu
 from jax.sharding import PartitionSpec as P
 
+
 CORES = 2
 LAYERS = 2
 NAMES = 3
+LATE = (1, 2)
 CHUNK = 32768
 VMEM_LIMIT = 4_000_000
 MESH = pl.DeviceIdType.MESH
@@ -49,8 +51,11 @@
 
 
 def kernel(n, *refs):
-    g, w, m, v, whole, new_m, new_v, own = (refs[i : i + NAMES] for i in range(0, 8 * NAMES, NAMES))
-    rs_send, rs_recv, pt_send, pt_recv, own_sem, mv_sem, w_sem, ag_send, ag_recv, pa_send, pa_recv, free, pt_free = refs[8 * NAMES :]
+    g, w, m, v, whole, new_m, new_v = (refs[i : i + NAMES] for i in range(0, 7 * NAMES, NAMES))
+    refs = refs[7 * NAMES :]
+    tails, refs = refs[: LAYERS * len(LATE)], refs[LAYERS * len(LATE) :]
+    own = refs[:NAMES]
+    rs_send, rs_recv, pt_send, pt_recv, own_sem, mv_sem, w_sem, tail_sem, ag_send, ag_recv, pa_send, pa_recv, free, pt_free = refs[NAMES:]
     chips = n // CORES
     last = chips - 1
     me = lax.axis_index("dp")
@@ -103,6 +108,10 @@
     def share(d, j, k):
         here = whole[j].at[place(d, j, k)]
         return remote(here, here, pa_send.at[d, j, k], pa_recv.at[d, j, k], partner)
+
+    def to_tail(d, j):
+        at = LATE.index(j) * LAYERS + d
+        return pltpu.make_async_copy(whole[j].at[place(d, j, last - 1)], tails[at], tail_sem.at[at])
 
     def allow(d, j, places):
         pl.semaphore_signal(free.at[d, j], inc=places, device_id={"dp": source[d]}, device_id_type=MESH)
@@ -176,7 +185,8 @@
             whole[j][spot(mine, at)] = new
 
         chunks(own[j].shape[1:], step)
-        allow_partner(d, j)
+        if j not in LATE:
+            allow_partner(d, j)
         ring(d, j, last - 2).wait_send()
         allow(d, j, 1)
         pl.semaphore_wait(free.at[d, j], 2)
@@ -184,37 +194,52 @@
         pl.semaphore_wait(pt_free.at[d, j], 1)
         share(d, j, 0).start()
 
-    def gather(k, more=True, lag=False):
+    def gather(k, lag=False):
         for d, j in pieces:
             pass_on(d, j, k - 1).wait_recv()
-            if more:
+            if isinstance(k, int) and k == last - 1 and j in LATE:
+                to_tail(d, j).start()
+            else:
                 pl.semaphore_wait(free.at[d, j], 1)
                 pass_on(d, j, k).start()
             pl.semaphore_wait(pt_free.at[d, j], 1)
             share(d, j, k).start()
             if lag:
                 ring(d, j, last - 1).wait_send()
-                allow(d, j, 2)
+                allow(d, j, 1 if j in LATE else 2)
 
     gather(1, lag=True)
 
-    @pl.loop(2, last)
+    @pl.loop(2, last - 1)
     def _(k):
         gather(k)
 
-    gather(last, more=False)
-
-    @pl.loop(0, chips)
+    gather(last - 1)
+    for d, j in pieces:
+        if j not in LATE:
+            pass_on(d, j, last - 1).wait_recv()
+            pl.semaphore_wait(pt_free.at[d, j], 1)
+            share(d, j, last).start()
+
+    @pl.loop(0, last - 1)
     def _(k):
         for d, j in pieces:
             to_partner(d, j, k).wait_send()
             share(d, j, k).wait_send()
             share(d, j, k).wait_recv()
-
-    @pl.loop(0, last)
-    def _(k):
-        for d, j in pieces:
             pass_on(d, j, k).wait_send()
+
+    for d, j in pieces:
+        to_partner(d, j, last - 1).wait_send()
+        to_partner(d, j, last).wait_send()
+        share(d, j, last - 1).wait_send()
+        share(d, j, last - 1).wait_recv()
+        if j in LATE:
+            to_tail(d, j).wait()
+        else:
+            pass_on(d, j, last - 1).wait_send()
+            share(d, j, last).wait_send()
+            share(d, j, last).wait_recv()
 
 
 def finish(*refs):
@@ -223,6 +248,32 @@
     for copy in copies:
         copy.start()
     for copy in copies:
+        copy.wait()
+
+
+def place_late(n, theirs, *refs):
+    count = LAYERS * len(LATE)
+    late, weights = refs[:count], refs[count + len(LATE) : count + 2 * len(LATE)]
+    bufs, sem = refs[count + 2 * len(LATE) : -1], refs[-1]
+    chips = n // CORES
+    me = lax.axis_index("dp")
+    core, chip = lax.rem(me, CORES), me // CORES
+    ins, outs = [], []
+    for i in range(count):
+        d, j = i % LAYERS, i // LAYERS
+        size = late[i].shape[0]
+        of_chip = lax.rem(chip + (1 if d == 0 else chips - 1), chips)
+        block = pl.ds(pl.multiple_of((of_chip * CORES + (1 - core if theirs else core)) * size, size), size)
+        if not theirs:
+            ins.append(pltpu.make_async_copy(late[i], bufs[i], sem.at[0, i]))
+        outs.append(pltpu.make_async_copy(late[i] if theirs else bufs[i], weights[j].at[d, block], sem.at[1, i]))
+    for copy in ins:
+        copy.start()
+    for i in range(count):
+        if not theirs:
+            ins[i].wait()
+        outs[i].start()
+    for copy in outs:
         copy.wait()
 
 
@@ -238,32 +289,53 @@
         credits = pltpu.SemaphoreType.REGULAR((LAYERS, NAMES))
         any_space, vmem = (pl.BlockSpec(memory_space=space) for space in (pl.ANY, pltpu.VMEM))
         results = (*weights, *m, *v)
+        late = [jax.ShapeDtypeStruct(blocks[j], jnp.bfloat16) for j in LATE for _ in range(LAYERS)]
         out = pl.pallas_call(
             functools.partial(kernel, n),
-            out_shape=[pltpu.VMEM(one.shape, one.dtype) for one in results],
+            out_shape=[pltpu.VMEM(one.shape, one.dtype) for one in results] + late,
             in_specs=[any_space] * (4 * NAMES),
-            out_specs=[vmem] * (3 * NAMES),
+            out_specs=[vmem] * (3 * NAMES) + [any_space] * len(late),
             scratch_shapes=[
                 *(pltpu.VMEM((LAYERS, *b), jnp.bfloat16) for b in blocks),
                 full, full, full, full,
-                sems(LAYERS, NAMES), sems(LAYERS, NAMES, 2), sems(LAYERS, NAMES),
+                sems(LAYERS, NAMES), sems(LAYERS, NAMES, 2), sems(LAYERS, NAMES), sems(len(late)),
                 full, full, full, full,
                 credits, credits,
             ],
             compiler_params=pltpu.CompilerParams(collective_id=0, has_side_effects=True, vmem_limit_bytes=VMEM_LIMIT),
             name="step",
         )(*terms, *weights, *m, *v)
-        return tuple(
-            pl.pallas_call(
-                finish,
-                out_shape=[jax.ShapeDtypeStruct(one.shape, one.dtype) for one in results],
-                in_specs=[vmem] * (3 * NAMES),
-                out_specs=[any_space] * (3 * NAMES),
-                scratch_shapes=[sems(3 * NAMES)],
+        hop = [[(i, (i + CORES) % n) for i in range(n)], [(i, (i - CORES) % n) for i in range(n)]]
+        come = []
+        for i, one in enumerate(out[3 * NAMES :]):
+            come.append(lax.ppermute(one, "dp", hop[i % LAYERS]))
+        across = []
+        for one in come:
+            across.append(lax.ppermute(one, "dp", [(i, i + 1 - 2 * (i % CORES)) for i in range(n)]))
+        done = pl.pallas_call(
+            finish,
+            out_shape=[jax.ShapeDtypeStruct(one.shape, one.dtype) for one in results],
+            in_specs=[vmem] * (3 * NAMES),
+            out_specs=[any_space] * (3 * NAMES),
+            scratch_shapes=[sems(3 * NAMES)],
+            compiler_params=pltpu.CompilerParams(vmem_limit_bytes=VMEM_LIMIT),
+            cost_estimate=pl.CostEstimate(flops=20_000_000_000, bytes_accessed=64_000_000, transcendentals=0),
+            name="finish",
+        )(*(pltpu.with_memory_space_constraint(one, pltpu.VMEM) for one in out[: 3 * NAMES]))
+        done = list(done)
+        for theirs, blocks_late, space in ((False, come, pltpu.HBM), (True, across, pltpu.VMEM)):
+            placed = pl.pallas_call(
+                functools.partial(place_late, n, theirs),
+                out_shape=[jax.ShapeDtypeStruct(done[j].shape, done[j].dtype) for j in LATE],
+                in_specs=[vmem if theirs else any_space] * len(late) + [any_space] * len(LATE),
+                out_specs=[any_space] * len(LATE),
+                scratch_shapes=[*([] if theirs else [pltpu.VMEM(one.shape, one.dtype) for one in late]), sems(2, len(late))],
+                input_output_aliases={len(late) + i: i for i in range(len(LATE))},
                 compiler_params=pltpu.CompilerParams(vmem_limit_bytes=VMEM_LIMIT),
-                name="finish",
-            )(*(pltpu.with_memory_space_constraint(one, pltpu.VMEM) for one in out))
-        )
+            )(*(pltpu.with_memory_space_constraint(one, space) for one in blocks_late), *(done[j] for j in LATE))
+            for j, one in zip(LATE, placed, strict=True):
+                done[j] = one
+        return tuple(done)
 
     all_of, cut = P(None, None, None), P(None, "dp", None)
     return jax.shard_map(

time: 511 us -> 522 us (1.022)
  waiting for transfers between devices: 0 us -> 19.2 us
  Pallas kernels: 510 us -> 493 us
  starting transfers between devices: 0 us -> 8.05 us
    pallas_call x1, Pallas kernels: 490 us -> 468 us  [step(): pl.pallas_call(functools.partial(kernel, n), out_shape=[pltpu.VMEM(one.sh...]
    ppermute x0 -> x8, waiting for transfers between devices: none -> 19.2 us  [the longest x4 19.1 us: step(): come.append(lax.ppermute(one, 'dp', hop[i % LAYERS]))]
    ppermute x0 -> x8, starting transfers between devices: none -> 8.05 us  [the longest x4 5.45 us: step(): come.append(lax.ppermute(one, 'dp', hop[i % LAYERS]))]
    pallas_call x0 -> x2, Pallas kernels: none -> 5.33 us  [step(): pl.pallas_call(functools.partial(place_late, n, theirs), out_shape=[jax.S...]
  transfers between devices with their start and end apart: 0 -> 8, of which waited for: 0 -> 2; matrix products, arithmetic and copies ran while one was open for 0% -> 0% of each run, Pallas kernels for 0% -> 4%
where the time goes in v3:
time: 522 us; the launch traced here: 521 us
  Pallas kernels  493 us (94%)
  waiting for transfers between devices  19.2 us (4%)
  starting transfers between devices  8.05 us (2%)
    pallas_call x1, Pallas kernels, step(): pl.pallas_call(functools.partial(kernel, n), out_shape=[pltpu.VMEM(one.sh...  468 us
    pallas_call x1, Pallas kernels, step(): pl.pallas_call(finish, out_shape=[jax.ShapeDtypeStruct(one.shape, one.dty...  20.2 us
    ppermute x4, waiting for transfers between devices, step(): come.append(lax.ppermute(one, 'dp', hop[i % LAYERS]))  19.1 us
  transfers between devices with their start and end apart: 8, of which 2 were waited for; matrix products, arithmetic and copies ran while one was open for 0% of the time, Pallas kernels for 4%

profile of v3, /device:TPU:21, one launch (start us, length us, event | category | flops | bytes accessed | tf_op | source)
XLA Modules:
  0.0 521.4 jit_solution(744442601704448727)
XLA Ops:
  0.6 468.0 %step.1 = (bf16[2,512,8192]{2,1,0:T(8,128)(2,1)S(1)}, bf16[2,512,8192]{2,1,0:T(8,128)(2,1)S(1)}, bf16[2,8192,512]{2,1,0:T(8,128)(2,1)S(1)}, f32[2,32,8192]{2,1,0...) custom-call(bf16[1,2,512,8192]{3,2,1,0:T(8,128)(2,1)} %refs_0_.1, ...), custom_call_target="tpu_custom_call" | custom-call | tf_op jit(solution)/shard_map/step/pallas_call | solution.py:293
  468.6 0.8 collective-permute-start
  469.4 2.0 collective-permute-start.2
  471.4 0.0 collective-permute-start.4
  471.4 2.7 collective-permute-start.6
  474.1 9.5 %collective-permute-done.refs_0_ = bf16[32,8192]{1,0:T(8,128)(2,1)} collective-permute-done((bf16[32,8192]{1,0:T(8,128)(2,1)}, bf16[32,8192]{1,0:T(8,128)(2,1)}, u32[]{:S(2)}, u32[]{:S(2)}) %collective-permute-start) | collective-permute-done | bytes 524320 | tf_op jit(solution)/shard_map/ppermute | solution.py:311
  483.6 1.6 collective-permute-start.1
  485.2 0.0 collective-permute-done.2.refs_1_
  485.2 0.0 collective-permute-start.3
  485.2 9.6 %collective-permute-done.4.refs_2_ = bf16[512,512]{1,0:T(8,128)(2,1)} collective-permute-done((bf16[512,512]{1,0:T(8,128)(2,1)}, bf16[512,512]{1,0:T(8,128)(2,1)}, u32[]{:S(2)}, u32[]{:S(2)}) %collective-permute-start.4) | collective-permute-done | bytes 524320 | tf_op jit(solution)/shard_map/ppermute | solution.py:311
  494.8 1.0 collective-permute-start.5
  495.8 0.0 collective-permute-done.6.refs_3_
  495.8 0.0 collective-permute-start.7
  495.8 20.2 %finish.1 = (bf16[2,512,8192]{2,1,0:T(8,128)(2,1)}, bf16[2,512,8192]{2,1,0:T(8,128)(2,1)}, bf16[2,8192,512]{2,1,0:T(8,128)(2,1)}, f32[2,32,8192]{2,1,0:T(8,128)}...) custom-call(bf16[2,512,8192]{2,1,0:T(8,128)(2,1)S(1)} %get-tuple-ele, ...), custom_call_target="tpu_custom_call" | custom-call | flops 20000000000 | bytes 64000000 | tf_op jit(solution)/shard_map/finish/pallas_call | solution.py:315
  516.0 2.4 shard_map.187
  518.4 0.0 collective-permute-done.1.refs_0_
  518.4 0.0 collective-permute-done.3.refs_1_
  518.4 0.0 collective-permute-done.5.refs_2_
  518.5 0.0 collective-permute-done.7.refs_3_
  518.5 2.9 shard_map.188
Async XLA Ops:
  468.6 15.0 %collective-permute-start = (bf16[32,8192]{1,0:T(8,128)(2,1)}, bf16[32,8192]{1,0:T(8,128)(2,1)}, u32[]{:S(2)}, u32[]{:S(2)}) collective-permute-start(bf16[32,8192]{1,0:T(8,128)(2,1)} %get-tuple-element.45), channel_id=1, source_target_pairs={{0,2},{1,3},{2,4},{3,5},{4,6},{5,7},{6,8},{7,9},{8,10},{9,11},{10,... | collective-permute-start | bytes 1572872 | tf_op jit(solution)/shard_map/ppermute | solution.py:311
  469.4 15.8 %collective-permute-start.2 = (bf16[32,8192]{1,0:T(8,128)(2,1)}, bf16[32,8192]{1,0:T(8,128)(2,1)}, u32[]{:S(2)}, u32[]{:S(2)}) collective-permute-start(bf16[32,8192]{1,0:T(8,128)(2,1)} %get-tuple-element.46), channel_id=1, source_target_pairs={{0,14},{1,15},{2,0},{3,1},{4,2},{5,3},{6,4},{7,5},{8,6},{9,7},{10,... | collective-permute-start | bytes 1572872 | tf_op jit(solution)/shard_map/ppermute | solution.py:311
  471.4 23.4 %collective-permute-start.4 = (bf16[512,512]{1,0:T(8,128)(2,1)}, bf16[512,512]{1,0:T(8,128)(2,1)}, u32[]{:S(2)}, u32[]{:S(2)}) collective-permute-start(bf16[512,512]{1,0:T(8,128)(2,1)} %get-tuple-element.47), channel_id=1, source_target_pairs={{0,2},{1,3},{2,4},{3,5},{4,6},{5,7},{6,8},{7,9},{8,10},{9,11},{10,... | collective-permute-start | bytes 1572872 | tf_op jit(solution)/shard_map/ppermute | solution.py:311
  471.4 24.4 %collective-permute-start.6 = (bf16[512,512]{1,0:T(8,128)(2,1)}, bf16[512,512]{1,0:T(8,128)(2,1)}, u32[]{:S(2)}, u32[]{:S(2)}) collective-permute-start(bf16[512,512]{1,0:T(8,128)(2,1)} %get-tuple-element.48), channel_id=1, source_target_pairs={{0,14},{1,15},{2,0},{3,1},{4,2},{5,3},{6,4},{7,5},{8,6},{9,7},{10,... | collective-permute-start | bytes 1572872 | tf_op jit(solution)/shard_map/ppermute | solution.py:311
  483.6 34.8 %collective-permute-start.1 = (bf16[32,8192]{1,0:T(8,128)(2,1)}, bf16[32,8192]{1,0:T(8,128)(2,1)}, u32[]{:S(2)}, u32[]{:S(2)}) collective-permute-start(bf16[32,8192]{1,0:T(8,128)(2,1)} %collective-permute-done.refs_0_), channel_id=1, source_target_pairs={{0,1},{1,0},{2,3},{3,2},{4,5},{5,4},{6,7},{7,6},{8,9},{9,8},{10,11... | collective-permute-start | bytes 1572872 | tf_op jit(solution)/shard_map/ppermute | solution.py:314
  485.2 33.3 %collective-permute-start.3 = (bf16[32,8192]{1,0:T(8,128)(2,1)}, bf16[32,8192]{1,0:T(8,128)(2,1)}, u32[]{:S(2)}, u32[]{:S(2)}) collective-permute-start(bf16[32,8192]{1,0:T(8,128)(2,1)} %collective-permute-done.2.refs_1_), channel_id=1, source_target_pairs={{0,1},{1,0},{2,3},{3,2},{4,5},{5,4},{6,7},{7,6},{8,9},{9,8},{10,11... | collective-permute-start | bytes 1572872 | tf_op jit(solution)/shard_map/ppermute | solution.py:314
  494.8 23.6 %collective-permute-start.5 = (bf16[512,512]{1,0:T(8,128)(2,1)}, bf16[512,512]{1,0:T(8,128)(2,1)}, u32[]{:S(2)}, u32[]{:S(2)}) collective-permute-start(bf16[512,512]{1,0:T(8,128)(2,1)} %collective-permute-done.4.refs_2_), channel_id=1, source_target_pairs={{0,1},{1,0},{2,3},{3,2},{4,5},{5,4},{6,7},{7,6},{8,9},{9,8},{10,11... | collective-permute-start | bytes 1572872 | tf_op jit(solution)/shard_map/ppermute | solution.py:314
  495.8 22.6 %collective-permute-start.7 = (bf16[512,512]{1,0:T(8,128)(2,1)}, bf16[512,512]{1,0:T(8,128)(2,1)}, u32[]{:S(2)}, u32[]{:S(2)}) collective-permute-start(bf16[512,512]{1,0:T(8,128)(2,1)} %collective-permute-done.6.refs_3_), channel_id=1, source_target_pairs={{0,1},{1,0},{2,3},{3,2},{4,5},{5,4},{6,7},{7,6},{8,9},{9,8},{10,11... | collective-permute-start | bytes 1572872 | tf_op jit(solution)/shard_map/ppermute | solution.py:314

commit v4 on v0

v4 whole, which is shorter than its diff:
```python
import functools

import jax
import jax.numpy as jnp
from jax import lax
from jax.experimental import pallas as pl
from jax.experimental.pallas import tpu as pltpu
from jax.sharding import PartitionSpec as P


CORES = 2
LAYERS = 2
NAMES = 3
ORDER = (2, 0, 1)
LATE = (0, 1)
END = ORDER[0]
SPLIT = 1
FIRST = 4
CHUNK = 32768
VMEM_LIMIT = 4_000_000
MESH = pl.DeviceIdType.MESH


def adamw(w, m, v, g):
    m = 0.9 * m + 0.1 * g
    v = 0.95 * v + 0.05 * g * g
    step = m * lax.rsqrt(v + 1e-8) + 0.1 * w
    return (w - 0.02 * step).astype(jnp.bfloat16), m, v


def chunks(shape, body):
    rows, columns = shape
    if columns * 16 <= CHUNK:
        size = min(rows, CHUNK // columns)

        @pl.loop(0, rows // size)
        def _(i):
            body((pl.ds(pl.multiple_of(i * size, size), size), slice(None)))
    else:
        size = min(columns, CHUNK // rows)

        @pl.loop(0, columns // size)
        def _(i):
            body((slice(None), pl.ds(pl.multiple_of(i * size, size), size)))


def spot(place, at):
    layer, block = place
    row, column = at
    if isinstance(row, slice):
        return layer, block, column
    return layer, pl.ds(pl.multiple_of(block.start + row.start, row.size), row.size), column


def kernel(n, *refs):
    g, w, m, v, whole, new_m, new_v = (refs[i : i + NAMES] for i in range(0, 7 * NAMES, NAMES))
    refs = refs[7 * NAMES :]
    tails, end, own, sems = refs[:LAYERS], refs[LAYERS], refs[LAYERS + 1 : LAYERS + 1 + NAMES], refs[LAYERS + 1 + NAMES :]
    rs_send, rs_recv, pt_send, pt_recv, first_recv, own_sem, m_sem, v_sem, w_sem, tail_sem, ag_send, ag_recv, pa_send, pa_recv, free, pt_free = sems
    chips = n // CORES
    last = chips - 1
    me = lax.axis_index("dp")
    core, chip = lax.rem(me, CORES), me // CORES
    partner = me + 1 - 2 * core
    up, down = lax.rem(me + CORES, n), lax.rem(me + n - CORES, n)
    to, source = (up, down), (down, up)
    pieces = [(d, (j, h)) for j in ORDER for h in range(SPLIT) for d in range(LAYERS)]

    def sem(array, d, p, *k):
        return array.at[(d, p[0] * SPLIT + p[1], *k)]

    def part(p):
        size = m[p[0]].shape[1] // SPLIT
        return pl.ds(p[1] * size, size)

    def rows(p, of_chip, of_core):
        j, h = p
        block = m[j].shape[1]
        size = block // SPLIT
        return pl.ds(pl.multiple_of((of_chip * CORES + of_core) * block + h * size, size), size)

    def sum_chip(d, k):
        return lax.rem(chip + 2 * chips - 1 - k, chips) if d == 0 else lax.rem(chip + 1 + k, chips)

    def place_chip(d, k):
        return lax.rem(chip + chips - k, chips) if d == 0 else lax.rem(chip + k, chips)

    def place(d, p, k):
        return d, rows(p, place_chip(d, k), core)

    def their_place(d, p, k):
        return d, rows(p, place_chip(d, k), 1 - core)

    def remote(src, dst, send, recv, device):
        return pltpu.make_async_remote_copy(src_ref=src, dst_ref=dst, send_sem=send, recv_sem=recv, device_id={"dp": device}, device_id_type=MESH)

    def to_partner(d, p, k):
        mine = g[p[0]].at[0, d, rows(p, sum_chip(d, k), 1 - core)]
        return remote(mine, whole[p[0]].at[place(d, p, k)], sem(pt_send, d, p, k), sem(pt_recv, d, p, k), partner)

    def quarter(block, s):
        size = block.size // FIRST
        return pl.ds(pl.multiple_of(block.start + s * size, size), size)

    def first_to_partner(d, p, s):
        j = p[0]
        mine = g[j].at[0, d, quarter(rows(p, sum_chip(d, 0), 1 - core), s)]
        there = whole[j].at[d, quarter(place(d, p, 0)[1], s)]
        return remote(mine, there, sem(pt_send, d, p, 0), first_recv.at[d, s], partner)

    def first_ring(d, p, s):
        here = whole[p[0]].at[d, quarter(place(d, p, 0)[1], s)]
        return remote(here, here, sem(rs_send, d, p, 0), sem(rs_recv, d, p, 1), to[d])

    def load_own(d, p, k):
        return pltpu.make_async_copy(g[p[0]].at[0, d, rows(p, sum_chip(d, k), core)], own[p[0]].at[d, part(p)], sem(own_sem, d, p))

    def load_w(d, p):
        return pltpu.make_async_copy(w[p[0]].at[d, rows(p, chip, core)], whole[p[0]].at[place(d, p, 0)], sem(w_sem, d, p))

    def load_moments(d, p):
        return (
            pltpu.make_async_copy(m[p[0]].at[d, part(p)], new_m[p[0]].at[d, part(p)], sem(m_sem, d, p)),
            pltpu.make_async_copy(v[p[0]].at[d, part(p)], new_v[p[0]].at[d, part(p)], sem(v_sem, d, p)),
        )

    def ring(d, p, k):
        here = whole[p[0]].at[place(d, p, k)]
        return remote(here, here, sem(rs_send, d, p, k), sem(rs_recv, d, p, k + 1), to[d])

    def pass_on(d, p, k):
        here = whole[p[0]].at[place(d, p, k)]
        return remote(here, here, sem(ag_send, d, p, k), sem(ag_recv, d, p, k + 1), to[d])

    def share(d, p, k):
        here = whole[p[0]].at[place(d, p, k)]
        return remote(here, here, sem(pa_send, d, p, k), sem(pa_recv, d, p, k), partner)

    def to_tail(d, p):
        return pltpu.make_async_copy(whole[p[0]].at[place(d, p, last - 1)], tails[d].at[LATE.index(p[0]), part(p)], sem(tail_sem, d, p))

    def last_hop(d, p):
        return remote(whole[p[0]].at[place(d, p, last - 1)], end.at[d, part(p)], sem(ag_send, d, p, last - 1), sem(ag_recv, d, p, last), to[d])

    def allow(d, p, places):
        pl.semaphore_signal(sem(free, d, p), inc=places, device_id={"dp": source[d]}, device_id_type=MESH)

    def allow_partner(d, p):
        pl.semaphore_signal(sem(pt_free, d, p), inc=1, device_id={"dp": partner}, device_id_type=MESH)

    barrier = pltpu.get_barrier_semaphore()
    for device in (up, down, partner):
        pl.semaphore_signal(barrier, inc=1, device_id={"dp": device}, device_id_type=MESH)
    for d, p in pieces:
        load_own(d, p, 0).start()
    pl.semaphore_wait(barrier, 3)

    def add(d, p, k, first, s=None):
        j = p[0]
        here, there, mine = place(d, p, k), their_place(d, p, k), (d, part(p))
        if s is not None:
            here, there, mine = ((layer, quarter(block, s)) for layer, block in (here, there, mine))

        def body(at):
            total = own[j][spot(mine, at)].astype(jnp.float32) + whole[j][spot(there, at)].astype(jnp.float32)
            if not first:
                total = total + whole[j][spot(here, at)].astype(jnp.float32)
            whole[j][spot(here, at)] = total.astype(jnp.bfloat16)

        chunks((here[1].size, own[j].shape[2]), body)

    def stage(k, first=False, lag=True):
        if not first:
            for d, p in pieces:
                to_partner(d, p, k + 1).start()
        for d, p in pieces[LAYERS:] if first else pieces:
            load_own(d, p, k).wait()
            to_partner(d, p, k).wait_recv()
            if not first:
                ring(d, p, k - 1).wait_recv()
            add(d, p, k, first)
            load_own(d, p, k + 1).start()
            ring(d, p, k).start()
            allow_partner(d, p)
            if lag:
                ring(d, p, k - 2).wait_send()
                allow(d, p, 1)

    for s in range(FIRST):
        for d, p in pieces[:LAYERS]:
            first_to_partner(d, p, s).start()
    for k in range(2):
        for d, p in pieces[LAYERS:] if k == 0 else pieces:
            to_partner(d, p, k).start()
    for s in range(FIRST):
        for d, p in pieces[:LAYERS]:
            if s == 0:
                load_own(d, p, 0).wait()
            first_to_partner(d, p, s).wait_recv()
            add(d, p, 0, True, s)
            first_ring(d, p, s).start()
    for d, p in pieces[:LAYERS]:
        load_own(d, p, 1).start()
        allow_partner(d, p)
    stage(0, first=True, lag=False)
    stage(1, lag=False)
    for d, p in pieces:
        for copy in load_moments(d, p):
            copy.start()

    @pl.loop(2, last)
    def _(k):
        stage(k)

    for d, p in pieces:
        load_w(d, p).start()
    for d, p in pieces:
        j = p[0]
        load_own(d, p, last).wait()
        to_partner(d, p, last).wait_recv()
        load_w(d, p).wait()
        for copy in load_moments(d, p):
            copy.wait()
        ring(d, p, last - 1).wait_recv()
        mine, here, there, block = place(d, p, 0), place(d, p, last), their_place(d, p, last), (d, part(p))

        def step(at, j=j, mine=mine, here=here, there=there, block=block):
            total = own[j][spot(block, at)].astype(jnp.float32) + whole[j][spot(there, at)].astype(jnp.float32)
            total = (total + whole[j][spot(here, at)].astype(jnp.float32)).astype(jnp.bfloat16).astype(jnp.float32)
            new, new_m[j][spot(block, at)], new_v[j][spot(block, at)] = adamw(
                whole[j][spot(mine, at)].astype(jnp.float32), new_m[j][spot(block, at)], new_v[j][spot(block, at)], total
            )
            whole[j][spot(mine, at)] = new

        chunks((here[1].size, own[j].shape[2]), step)
        ring(d, p, last - 2).wait_send()
        allow(d, p, 1)
        pl.semaphore_wait(sem(free, d, p), 2)
        pass_on(d, p, 0).start()
        pl.semaphore_wait(sem(pt_free, d, p), 1)
        share(d, p, 0).start()

    def gather(k, lag=False, final=False):
        for d, p in pieces:
            pass_on(d, p, k - 1).wait_recv()
            if final and p[0] == END:
                last_hop(d, p).start()
            elif final:
                to_tail(d, p).start()
            else:
                pl.semaphore_wait(sem(free, d, p), 1)
                pass_on(d, p, k).start()
            pl.semaphore_wait(sem(pt_free, d, p), 1)
            share(d, p, k).start()
            if lag:
                ring(d, p, last - 1).wait_send()
                allow(d, p, 1)

    gather(1, lag=True)

    @pl.loop(2, last - 1)
    def _(k):
        gather(k)

    gather(last - 1, final=True)

    @pl.loop(0, last - 1)
    def _(k):
        for d, p in pieces:
            to_partner(d, p, k).wait_send()
            share(d, p, k).wait_send()
            share(d, p, k).wait_recv()
            pass_on(d, p, k).wait_send()

    for d, p in pieces:
        to_partner(d, p, last - 1).wait_send()
        to_partner(d, p, last).wait_send()
        share(d, p, last - 1).wait_send()
        share(d, p, last - 1).wait_recv()
        if p[0] in LATE:
            to_tail(d, p).wait()
    for d, p in pieces:
        if p[0] == END:
            last_hop(d, p).wait_send()
            last_hop(d, p).wait_recv()


def finish(n, *refs):
    count = (len(refs) - 1) // 2
    ins, outs, sem = refs[:count], refs[count : 2 * count], refs[-1]
    chips = n // CORES
    chip = lax.axis_index("dp") // CORES
    copies = []
    for j in range(count):
        for d in range(LAYERS):
            if j < NAMES:
                size = ins[j].shape[1] // chips
                for k in range(chips - 1):
                    at = d, pl.ds(pl.multiple_of(lax.rem(chip + (chips - k if d == 0 else k), chips) * size, size), size)
                    copies.append((ins[j].at[at], outs[j].at[at]))
            else:
                copies.append((ins[j].at[d], outs[j].at[d]))
    copies = [pltpu.make_async_copy(*one, sem.at[i]) for i, one in enumerate(copies)]
    for copy in copies:
        copy.start()
    for copy in copies:
        copy.wait()


def place_late(n, items, arrays, weights, *refs):
    late, out = refs[:arrays], refs[arrays + weights : arrays + 2 * weights]
    bufs, sem = refs[arrays + 2 * weights : -1], refs[-1]
    chips = n // CORES
    me = lax.axis_index("dp")
    core, chip = lax.rem(me, CORES), me // CORES
    ins, outs = [], []
    for x, (array, i, theirs, weight, d) in enumerate(items):
        size = late[array].shape[1]
        of_chip = lax.rem(chip + (1 if d == 0 else chips - 1), chips)
        block = pl.ds(pl.multiple_of((of_chip * CORES + (1 - core if theirs else core)) * size, size), size)
        if bufs:
            ins.append(pltpu.make_async_copy(late[array].at[i], bufs[0].at[x], sem.at[0, x]))
        outs.append(pltpu.make_async_copy(bufs[0].at[x] if bufs else late[array].at[i], out[weight].at[d, block], sem.at[1, x]))
    for copy in ins:
        copy.start()
    for x, copy in enumerate(outs):
        if bufs:
            ins[x].wait()
        copy.start()
    for copy in outs:
        copy.wait()


def solution(mesh):
    n = mesh.shape["dp"]
    chips = n // CORES

    def step(*arrays):
        terms, weights, m, v = (arrays[i : i + NAMES] for i in range(0, 4 * NAMES, NAMES))
        blocks = [one.shape[1:] for one in m]
        sems = lambda *shape: pltpu.SemaphoreType.DMA(shape)
        one_each, full = sems(LAYERS, NAMES * SPLIT), sems(LAYERS, NAMES * SPLIT, chips)
        credits = pltpu.SemaphoreType.REGULAR((LAYERS, NAMES * SPLIT))
        any_space, vmem = (pl.BlockSpec(memory_space=space) for space in (pl.ANY, pltpu.VMEM))
        results = (*weights, *m, *v)
        late = [jax.ShapeDtypeStruct((len(LATE), *blocks[LATE[0]]), jnp.bfloat16)] * LAYERS
        late.append(jax.ShapeDtypeStruct((LAYERS, *blocks[END]), jnp.bfloat16))
        out = pl.pallas_call(
            functools.partial(kernel, n),
            out_shape=[pltpu.VMEM(one.shape, one.dtype) for one in results] + late,
            in_specs=[any_space] * (4 * NAMES),
            out_specs=[vmem] * (3 * NAMES) + [any_space] * len(late),
            scratch_shapes=[
                *(pltpu.VMEM((LAYERS, *b), jnp.bfloat16) for b in blocks),
                full, full, full, full,
                sems(LAYERS, FIRST), one_each, one_each, one_each, one_each, one_each,
                full, full, full, full,
                credits, credits,
            ],
            compiler_params=pltpu.CompilerParams(collective_id=0, has_side_effects=True, vmem_limit_bytes=VMEM_LIMIT),
            name="step",
        )(*terms, *weights, *m, *v)

        def hop(i, one):
            by = CORES if i == 0 else n - CORES
            return lax.ppermute(one, "dp", [(a, (a + by) % n) for a in range(n)])

        def across(one):
            return lax.ppermute(one, "dp", [(a, a + 1 - 2 * (a % CORES)) for a in range(n)])

        *tails, end = out[3 * NAMES :]
        come = [hop(i, one) for i, one in enumerate(tails)]
        ends = [end, across(end)]
        shared = [across(one) for one in come]
        done = pl.pallas_call(
            functools.partial(finish, n),
            out_shape=[jax.ShapeDtypeStruct(one.shape, one.dtype) for one in results],
            in_specs=[vmem] * (3 * NAMES),
            out_specs=[any_space] * (3 * NAMES),
            scratch_shapes=[sems(LAYERS * NAMES * (chips + 1))],
            compiler_params=pltpu.CompilerParams(vmem_limit_bytes=VMEM_LIMIT),
            cost_estimate=pl.CostEstimate(flops=20_000_000_000, bytes_accessed=64_000_000, transcendentals=0),
            name="finish",
        )(*(pltpu.with_memory_space_constraint(one, pltpu.VMEM) for one in out[: 3 * NAMES]))
        done = list(done)

        def place(js, sources, space, items):
            blocks_late = [pltpu.with_memory_space_constraint(one, space) for one in sources]
            bounce = [pltpu.VMEM((len(items), *sources[0].shape[1:]), jnp.bfloat16)] if space is pltpu.HBM else []
            placed = pl.pallas_call(
                functools.partial(place_late, n, items, len(sources), len(js)),
                out_shape=[jax.ShapeDtypeStruct(done[j].shape, done[j].dtype) for j in js],
                in_specs=[any_space if bounce else vmem] * len(sources) + [any_space] * len(js),
                out_specs=[any_space] * len(js),
                scratch_shapes=[*bounce, sems(2, len(items))],
                input_output_aliases={len(sources) + i: i for i in range(len(js))},
                compiler_params=pltpu.CompilerParams(vmem_limit_bytes=VMEM_LIMIT),
            )(*blocks_late, *(done[j] for j in js))
            for j, one in zip(js, placed, strict=True):
                done[j] = one

        place((END,), ends, pltpu.HBM, [(i, d, i == 1, 0, d) for i in range(2) for d in range(LAYERS)])
        place(LATE, come, pltpu.HBM, [(d, i, False, i, d) for i in range(len(LATE)) for d in range(LAYERS)])
        place(LATE, shared, pltpu.VMEM, [(d, i, True, i, d) for i in range(len(LATE)) for d in range(LAYERS)])
        return tuple(done)

    all_of, cut = P(None, None, None), P(None, "dp", None)
    return jax.shard_map(
        step,
        mesh=mesh,
        in_specs=(P(("rep", "dp"), None, None, None),) * 3 + (all_of,) * 3 + (cut,) * 6,
        out_specs=(P("rep", None, None),) * 3 + (P("rep", "dp", None),) * 6,
        check_vma=False,
    )
```

time: 629 us -> 519 us (0.83)
  waiting for transfers between devices: 564 us -> 22.2 us
  Pallas kernels: 0 us -> 491 us
  local copies, waits for them, and re-layouts: 34.1 us -> 0 us
  other arithmetic: 16.2 us -> 0 us
  between operations: 14.2 us -> 0.71 us
    pallas_call x0 -> x5, Pallas kernels: none -> 491 us  [the longest x1 465 us: step(): pl.pallas_call(functools.partial(kernel, n), out_shape=[pltpu.VMEM(one.sh...]
    reduce_scatter x3 -> x0, waiting for transfers between devices: 287 us -> none  [step(): lax.psum_scatter(t[0], 'dp', scatter_dimension=1, tiled=True)]
    all_gather x3 -> x0, waiting for transfers between devices: 274 us -> none  [step(): whole = [lax.all_gather(one[0], 'dp', axis=1, tiled=True) for one in new]]
    unnamed x17 -> x0, local copies, waits for them, and re-layouts: 34.1 us -> none
    ppermute x0 -> x5, waiting for transfers between devices: none -> 22.2 us  [the longest x2 22.2 us: hop(): return lax.ppermute(one, 'dp', [(a, (a + by) % n) for a in range(n)])]
    convert_element_type x3 -> x0, other arithmetic: 16.2 us -> none  [adamw(): return ((w - 0.02 * step).astype(jnp.bfloat16), m, v)]
  transfers between devices with their start and end apart: 6 -> 5, of which waited for: 6 -> 1; matrix products, arithmetic and copies ran while one was open for 3% -> 0% of each run, Pallas kernels for 0% -> 4%
where the time goes in v4:
time: 519 us
  Pallas kernels  491 us (95%)
  waiting for transfers between devices  22.2 us (4%)
    pallas_call x1, Pallas kernels, step(): pl.pallas_call(functools.partial(kernel, n), out_shape=[pltpu.VMEM(one.sh...  465 us
    ppermute x2, waiting for transfers between devices, hop(): return lax.ppermute(one, 'dp', [(a, (a + by) % n) for a in range(n)])  22.2 us
    pallas_call x1, Pallas kernels, step(): pl.pallas_call(functools.partial(finish, n), out_shape=[jax.ShapeDtypeStr...  18.3 us
  transfers between devices with their start and end apart: 5, of which 1 were waited for; matrix products, arithmetic and copies ran while one was open for 0% of the time, Pallas kernels for 4%

profile of v4, /device:TPU:21, one launch (start us, length us, event | category | flops | bytes accessed | tf_op | source)
XLA Modules:
  0.0 518.9 jit_solution(10091790902260802772)
XLA Ops:
  0.6 464.9 %step.1 = (bf16[2,512,8192]{2,1,0:T(8,128)(2,1)S(1)}, bf16[2,512,8192]{2,1,0:T(8,128)(2,1)S(1)}, bf16[2,8192,512]{2,1,0:T(8,128)(2,1)S(1)}, f32[2,32,8192]{2,1,0...) custom-call(bf16[1,2,512,8192]{3,2,1,0:T(8,128)(2,1)} %refs_0_.1, ...), custom_call_target="tpu_custom_call" | custom-call | tf_op jit(solution)/shard_map/step/pallas_call | solution.py:348
  465.5 0.8 collective-permute-start
  466.3 2.0 collective-permute-start.2
  468.3 1.0 collective-permute-start.4
  469.3 22.2 %collective-permute-done.refs_0_ = bf16[2,32,8192]{2,1,0:T(8,128)(2,1)} collective-permute-done((bf16[2,32,8192]{2,1,0:T(8,128)(2,1)}, bf16[2,32,8192]{2,1,0:T(8,128)(2,1)}, u32[]{:S(2)}, u32[]{:S(2)}) %collective-permute-start) | collective-permute-done | bytes 1048608 | tf_op jit(solution)/shard_map/ppermute | solution.py:366
  491.5 1.3 collective-permute-start.1
  492.7 0.0 collective-permute-done.2.refs_1_
  492.7 0.0 collective-permute-start.3
  492.8 18.3 %finish.1 = (bf16[2,512,8192]{2,1,0:T(8,128)(2,1)}, bf16[2,512,8192]{2,1,0:T(8,128)(2,1)}, bf16[2,8192,512]{2,1,0:T(8,128)(2,1)}, f32[2,32,8192]{2,1,0:T(8,128)}...) custom-call(bf16[2,512,8192]{2,1,0:T(8,128)(2,1)S(1)} %get-tuple-ele, ...), custom_call_target="tpu_custom_call" | custom-call | flops 20000000000 | bytes 64000000 | tf_op jit(solution)/shard_map/finish/pallas_call | solution.py:375
  511.0 0.0 collective-permute-done.4.refs_1_
  511.1 2.4 shard_map.189
  513.5 2.4 shard_map.187
  515.9 0.0 collective-permute-done.1.refs_0_
  515.9 0.0 collective-permute-done.3.refs_1_
  515.9 2.9 shard_map.188
Async XLA Ops:
  465.5 25.9 %collective-permute-start = (bf16[2,32,8192]{2,1,0:T(8,128)(2,1)}, bf16[2,32,8192]{2,1,0:T(8,128)(2,1)}, u32[]{:S(2)}, u32[]{:S(2)}) collective-permute-start(bf16[2,32,8192]{2,1,0:T(8,128)(2,1)} %get-tuple-element.34), channel_id=1, source_target_pairs={{0,2},{1,3},{2,4},{3,5},{4,6},{5,7},{6,8},{7,9},{8,10},{9,11},{10,... | collective-permute-start | bytes 3145736 | tf_op jit(solution)/shard_map/ppermute | solution.py:366
  466.3 26.4 %collective-permute-start.2 = (bf16[2,32,8192]{2,1,0:T(8,128)(2,1)}, bf16[2,32,8192]{2,1,0:T(8,128)(2,1)}, u32[]{:S(2)}, u32[]{:S(2)}) collective-permute-start(bf16[2,32,8192]{2,1,0:T(8,128)(2,1)} %get-tuple-element.35), channel_id=1, source_target_pairs={{0,14},{1,15},{2,0},{3,1},{4,2},{5,3},{6,4},{7,5},{8,6},{9,7},{10,... | collective-permute-start | bytes 3145736 | tf_op jit(solution)/shard_map/ppermute | solution.py:366
  468.3 42.7 %collective-permute-start.4 = (bf16[2,512,512]{2,1,0:T(8,128)(2,1)}, bf16[2,512,512]{2,1,0:T(8,128)(2,1)}, u32[]{:S(2)}, u32[]{:S(2)}) collective-permute-start(bf16[2,512,512]{2,1,0:T(8,128)(2,1)} %get-tuple-element.51.refs_0_), channel_id=1, source_target_pairs={{0,1},{1,0},{2,3},{3,2},{4,5},{5,4},{6,7},{7,6},{8,9},{9,8},{10,11... | collective-permute-start | bytes 3145736 | tf_op jit(solution)/shard_map/ppermute | solution.py:369
  491.5 24.4 %collective-permute-start.1 = (bf16[2,32,8192]{2,1,0:T(8,128)(2,1)}, bf16[2,32,8192]{2,1,0:T(8,128)(2,1)}, u32[]{:S(2)}, u32[]{:S(2)}) collective-permute-start(bf16[2,32,8192]{2,1,0:T(8,128)(2,1)} %collective-permute-done.refs_0_), channel_id=1, source_target_pairs={{0,1},{1,0},{2,3},{3,2},{4,5},{5,4},{6,7},{7,6},{8,9},{9,8},{10,11... | collective-permute-start | bytes 3145736 | tf_op jit(solution)/shard_map/ppermute | solution.py:369
  492.7 23.2 %collective-permute-start.3 = (bf16[2,32,8192]{2,1,0:T(8,128)(2,1)}, bf16[2,32,8192]{2,1,0:T(8,128)(2,1)}, u32[]{:S(2)}, u32[]{:S(2)}) collective-permute-start(bf16[2,32,8192]{2,1,0:T(8,128)(2,1)} %collective-permute-done.2.refs_1_), channel_id=1, source_target_pairs={{0,1},{1,0},{2,3},{3,2},{4,5},{5,4},{6,7},{7,6},{8,9},{9,8},{10,11... | collective-permute-start | bytes 3145736 | tf_op jit(solution)/shard_map/ppermute | solution.py:369
